TPU v7x, 512 devices: a 4x2x32 block of a 4x8x32 slice. The times are simulated.
512 devices in a mesh: grp: 2 (over y), user: 64 (over z, core), head: 4 (over x).
Axes of the slice: x: 4, y: 2, z: 32, core: 2. Of those that a mesh axis runs over, the one named last changes fastest.
The devices are a block of a 4x8x32 slice.
Arguments:
- cand_ids: int32 [128, 512], P(('grp', 'user')), parts along dimension 0, may hold values from 0 to 32767, as said below
- prefix_len: int32 [128], P(('grp', 'user')), parts along dimension 0, may hold values from 1 to 512
- key_cache: bfloat16 [128, 512, 1024], P(('grp', 'user'), None, 'head'), parts along dimension 0, may hold values from -6 to 6
- value_cache: bfloat16 [128, 512, 1024], P(('grp', 'user'), None, 'head'), parts along dimension 0, may hold values from -6 to 6
- item_table: bfloat16 [32768, 1024], P('user'), may hold values from -6 to 6
- w_qkvu: bfloat16 [1024, 8, 4, 128], P(None, 'head'), may hold values from -0.1875 to 0.1875
- w_out: bfloat16 [8, 128, 1024], P('head'), may hold values from -0.1875 to 0.1875
Outputs:
- scores: float32 [128, 512], P(('grp', 'user')), parts along dimension 0
There are 2 independent parts, one for each index of `grp`. A program takes and returns all parts, laid end to end along the dimension named above; an argument that names none is the same for every part. Nothing has to cross between parts.
Inputs may be any that keep to these rules, and one draw needn't show every extreme that they name: `cand_ids`: item id s * 512 + r lies in table shard s. Among the 512 candidates of each aligned block of 1 users, at most 16 lie in one table shard, and in every block some shard holds exactly 16 of them.
All inputs are finite; a program needn't handle non-finite values.
Results may differ from a plain program's by a relative error of at most 0.0095.
Values may be sent and summed in bfloat16 or wider, within the bound.
A program may use at most 64 MiB of HBM per device.

v0:
```python
import jax
import jax.numpy as jnp
from jax import lax
from jax.sharding import Mesh
from jax.sharding import PartitionSpec as P

USER = ("user_0", "user_1")
GRP_USER = ("grp", "user_0", "user_1")


def cut_along(x, dim, length):
    lengths = x.shape
    pieces = x.reshape(*lengths[:dim], length, lengths[dim] // length, *lengths[dim + 1 :])
    return jnp.moveaxis(pieces, dim, 0)


def in_order(pieces, dim):
    lengths = list(pieces.shape[1:])
    lengths[dim] *= pieces.shape[0]
    return jnp.moveaxis(pieces, 0, dim).reshape(lengths)


def moved_by_axis(pieces, axes, order):
    lengths = [lax.axis_size(a) for a in axes]
    pieces = pieces.reshape(*lengths, *pieces.shape[1:])
    for k in order:
        pieces = lax.all_to_all(pieces, axes[k], split_axis=k, concat_axis=k, tiled=True)
    return pieces.reshape(-1, *pieces.shape[len(axes) :])


def one_axis_at_a_time(x, axes, order, split_dim, concat_dim):
    pieces = cut_along(x, split_dim, lax.axis_size(axes))
    return in_order(moved_by_axis(pieces, axes, order), concat_dim)


def from_everyone(x, axis):
    copies = jnp.broadcast_to(x, (lax.axis_size(axis), *x.shape))
    return lax.all_to_all(copies, axis, split_axis=0, concat_axis=0, tiled=True)


def gathered_copies(x, axis, dim):
    pieces = from_everyone(x, axis)
    return in_order(pieces, dim)


def sent_and_summed(x, axis, dim):
    pieces = cut_along(x, dim, lax.axis_size(axis))
    arrived = lax.all_to_all(pieces, axis, split_axis=0, concat_axis=0, tiled=True)
    return arrived.astype(jnp.float32).sum(axis=0)


def of_everyone(x, axis):
    everything = from_everyone(x, axis)
    return jnp.sum(everything, axis=0)


def together(arrays, axis):
    ravelled, at, gathered = (jnp.concatenate([a.reshape(-1) for a in arrays]), 0, [])
    subtotal = of_everyone(ravelled, axis)
    for a in arrays:
        gathered.append(subtotal[at : at + a.size].reshape(a.shape))
        at += a.size
    return tuple(gathered)


def body(cand_ids, prefix_len, key_cache, value_cache, item_table, w_qkvu, w_out):
    user_count, cand_count = cand_ids.shape
    model_width = item_table.shape[1]
    heads_here = w_qkvu.shape[1]
    head_size = w_qkvu.shape[3]
    prefix_most = key_cache.shape[1]
    score_scale = head_size ** (-0.5)
    shard_count = lax.axis_size(USER)
    rows_shard = item_table.shape[0]
    item_ids = cand_ids.reshape(-1)
    row_count = item_ids.shape[0]
    capacity = 2 * row_count // shard_count
    shard_of = item_ids // rows_shard
    local_row = item_ids - shard_of * rows_shard
    one_hot = (shard_of[:, None] == jnp.arange(shard_count, dtype=jnp.int32)[None, :]).astype(
        jnp.int32
    )
    position = jnp.sum((jnp.cumsum(one_hot, axis=0) - 1) * one_hot, axis=1)
    slot_index = shard_of * capacity + position
    requests = jnp.full((shard_count * capacity,), -1, jnp.int32).at[slot_index].set(local_row)
    received = one_axis_at_a_time(requests.reshape(shard_count, capacity), USER, (0, 1), 0, 0)
    safe_rows = jnp.maximum(received.reshape(-1), 0)
    col_width = model_width // lax.axis_size("head")
    head_index = lax.axis_index("head")
    table_cols = lax.dynamic_slice_in_dim(item_table, head_index * col_width, col_width, 1)
    looked_up = table_cols[safe_rows].reshape(shard_count, capacity, col_width)
    returned = lax.all_to_all(looked_up, USER, split_axis=0, concat_axis=0, tiled=True)
    own_cols = returned.reshape(-1, col_width)[slot_index]
    embedded = gathered_copies(own_cols, "head", 1)
    projected = jnp.dot(
        embedded, w_qkvu.reshape(model_width, -1), preferred_element_type=jnp.float32
    )
    activated = jax.nn.silu(projected).astype(jnp.bfloat16)
    activated = activated.reshape(user_count, cand_count, heads_here, 4, head_size)
    queries = activated[:, :, :, 0]
    own_keys = activated[:, :, :, 1]
    own_values = activated[:, :, :, 2]
    gates = activated[:, :, :, 3]
    cached_keys = key_cache.reshape(user_count, prefix_most, heads_here, head_size)
    cached_values = value_cache.reshape(user_count, prefix_most, heads_here, head_size)
    raw = jnp.einsum("uchd,uphd->uhcp", queries, cached_keys, preferred_element_type=jnp.float32)
    denominator = (prefix_len + 1).astype(jnp.float32)
    in_prefix = jnp.arange(prefix_most, dtype=jnp.int32)[None, :] < prefix_len[:, None]
    weights = jnp.where(in_prefix[:, None, None, :], jax.nn.silu(raw * score_scale), 0.0)
    weights = (weights / denominator[:, None, None, None]).astype(jnp.bfloat16)
    attended = jnp.einsum(
        "uhcp,uphd->uchd", weights, cached_values, preferred_element_type=jnp.float32
    )
    own_dot = jnp.sum(queries.astype(jnp.float32) * own_keys.astype(jnp.float32), axis=-1)
    own_weight = jax.nn.silu(own_dot * score_scale) / denominator[:, None, None]
    attended = attended + own_weight[..., None] * own_values.astype(jnp.float32)
    mean_square = jnp.mean(attended * attended, axis=-1, keepdims=True)
    gated = (attended * lax.rsqrt(mean_square + 1e-06) * gates.astype(jnp.float32)).astype(
        jnp.bfloat16
    )
    partial_value = jnp.dot(
        gated.reshape(row_count, heads_here * head_size),
        w_out.reshape(heads_here * head_size, model_width),
        preferred_element_type=jnp.float32,
    )
    col_width = model_width // lax.axis_size("head")
    head_index = lax.axis_index("head")
    summed_cols = sent_and_summed(partial_value.astype(jnp.bfloat16), "head", 1)
    embed_cols = lax.dynamic_slice_in_dim(embedded, head_index * col_width, col_width, 1).astype(
        jnp.float32
    )
    square_part = jnp.sum(summed_cols * summed_cols, axis=1)
    inner_part = jnp.sum(summed_cols * embed_cols, axis=1)
    square_total, inner_total = together((square_part, inner_part), "head")
    scores_out = inner_total * model_width ** (-0.5) * lax.rsqrt(square_total / model_width + 1e-06)
    return scores_out.reshape(user_count, cand_count)


def solution(mesh):
    split = Mesh(
        mesh.devices.reshape(mesh.shape["grp"], 32, 2, mesh.shape["head"]),
        ("grp", "user_0", "user_1", "head"),
    )
    in_specs = (
        P(GRP_USER, None),
        P(GRP_USER),
        P(GRP_USER, None, "head"),
        P(GRP_USER, None, "head"),
        P(USER, None),
        P(None, "head", None, None),
        P("head", None, None),
    )
    out_specs = P(GRP_USER, None)
    return jax.shard_map(body, mesh=split, in_specs=in_specs, out_specs=out_specs, check_vma=False)
```

profile of v0, /device:TPU:104, one launch (start us, length us, event | category | flops | bytes accessed | tf_op | source)
XLA Modules:
  0.0 217.8 jit_solution(9184464155357843166)
XLA Ops:
  0.0 0.0 copy-start
  0.0 0.8 add_select_fusion
  0.8 1.2 reduce-window.6
  2.0 0.2 slice_reduce_fusion
  2.3 0.7 multiply_subtract_fusion
  3.0 0.1 fusion.14
  3.1 0.7 compare_select_fusion
  3.8 2.4 %scatter_custom_fusion = s32[1024]{0:T(1024)S(1)} fusion(s32[512]{0:T(512)S(1)} %bitcast.88, s32[512]{0:T(512)S(1)} %get-tuple-element.11, s32[]{:T(128)} %constant.23.clone.1), kind=kCustom, calls=%fused_computation.61 | custom fusion | bytes 4100 | tf_op jit(solution)/shard_map/scatter | solution.py:85
  6.3 0.7 reshape_reshape_reshape.4
  7.0 44.3 %all-to-all-start = ((s32[32,2,1,16]{3,1,2,0:T(2,128)}), s32[32,2,1,16]{3,1,2,0:T(2,128)S(1)}, u32[]{:S(2)}, u32[]{:S(2)}) async-start(s32[32,2,1,16]{3,1,2,0:T(2,128)} %bitcast.7), calls=%async_computation | async-start | bytes 65536 | tf_op jit(solution)/shard_map/all_to_all | solution.py:27
  51.3 0.0 copy-done
  51.3 21.6 %all-to-all-done = s32[32,2,1,16]{3,1,2,0:T(2,128)S(1)} async-done(((s32[32,2,1,16]{3,1,2,0:T(2,128)}), s32[32,2,1,16]{3,1,2,0:T(2,128)S(1)}, u32[]{:S(2)}, u32[]{:S(2)}) %all-to-all-start) | async-done | bytes 4128 | tf_op jit(solution)/shard_map/all_to_all | solution.py:27
  72.9 0.1 copy.52
  73.0 0.1 reshape.357
  73.1 3.7 %all_to_all.31 = s32[2,1,512]{2,1,0:T(1,128)S(1)} all-to-all(s32[2,1,512]{2,1,0:T(1,128)S(1)} %reshape.357), channel_id=1, replica_groups=mesh['grp'=2,'user_0'=32,'user_1'=2,'head'=4] {'user_1'}, dimensions={0} | all-to-all | bytes 8192 | tf_op jit(solution)/shard_map/all_to_all | solution.py:27
  76.8 0.5 broadcast.252
  77.3 0.7 reduce.6
  78.0 0.1 reshape.358
  78.1 0.1 copy.53
  78.2 0.1 reshape.331
  78.3 4.9 %gather_fusion = bf16[1024,256]{1,0:T(8,128)(2,1)} fusion(bf16[512,256]{1,0:T(8,128)(2,1)S(1)} %constant_dynamic-slice_fusion.1, s32[1024]{0:T(1024)S(1)} %broadcast_clamp_fusion), kind=kCustom, calls=%fused_computation | custom fusion | bytes 1052672 | tf_op jit(solution)/shard_map/gather | solution.py:91
  83.2 6.4 %all-to-all-start.2 = ((bf16[64,16,256]{2,1,0:T(8,128)(2,1)}), bf16[64,16,256]{2,1,0:T(8,128)(2,1)S(1)}, u32[]{:S(2)}, u32[]{:S(2)}) async-start(bf16[64,16,256]{2,1,0:T(8,128)(2,1)} %bitcast.8), calls=%async_computation.2 | async-start | bytes 1048576 | tf_op jit(solution)/shard_map/all_to_all | solution.py:92
  89.6 64.5 %all-to-all-done.2 = bf16[64,16,256]{2,1,0:T(8,128)(2,1)S(1)} async-done(((bf16[64,16,256]{2,1,0:T(8,128)(2,1)}), bf16[64,16,256]{2,1,0:T(8,128)(2,1)S(1)}, u32[]{:S(2)}, u32[]{:S(2)}) %all-to-all-start.2) | async-done | bytes 524320 | tf_op jit(solution)/shard_map/all_to_all | solution.py:92
  154.1 2.6 %gather_fusion.1 = bf16[512,256]{1,0:T(8,128)(2,1)} fusion(bf16[1024,256]{1,0:T(8,128)(2,1)S(1)} %bitcast.79, s32[1024]{0:T(1024)S(1)} %pad_clamp_fusion), kind=kCustom, calls=%fused_computation.1 | custom fusion | bytes 526336 | tf_op jit(solution)/shard_map/gather | solution.py:93
  156.7 0.0 copy-start.1
  156.7 1.2 copy.54
  158.0 1.1 broadcast_in_dim.20
  159.0 4.6 %all-to-all-start.3 = ((bf16[4,512,256]{1,2,0:T(8,128)(2,1)}), bf16[4,512,256]{1,2,0:T(8,128)(2,1)}, u32[]{:S(2)}, u32[]{:S(2)}) async-start(bf16[4,512,256]{1,2,0:T(8,128)(2,1)} %broadcast_in_dim.20), calls=%async_computation.3 | async-start | bytes 2097152 | tf_op jit(solution)/shard_map/all_to_all | solution.py:38
  163.6 0.0 copy-done.1
  163.6 0.0 copy-start.3
  163.6 2.7 %reshape.318 = bf16[1024,1024]{1,0:T(8,128)(2,1)} reshape(bf16[1024,2,4,128]{3,2,1,0:T(4,128)(2,1)S(1)} %copy-done.1) | data formatting | bytes 4194304 | tf_op jit(solution)/shard_map/reshape | solution.py:96
  167.0 0.0 copy-done.3
  167.0 0.8 copy.65
  167.8 1.7 reshape.321
  169.5 8.6 %all-to-all-done.3 = bf16[4,512,256]{1,2,0:T(8,128)(2,1)} async-done(((bf16[4,512,256]{1,2,0:T(8,128)(2,1)}), bf16[4,512,256]{1,2,0:T(8,128)(2,1)}, u32[]{:S(2)}, u32[]{:S(2)}) %all-to-all-start.3) | async-done | bytes 1048608 | tf_op jit(solution)/shard_map/all_to_all | solution.py:38
  178.2 3.5 %multiply_convert_fusion = bf16[512,1024]{1,0:T(8,128)(2,1)S(1)} fusion(bf16[512,1024]{0,1:T(8,128)(2,1)} %bitcast.11, bf16[1024,1024]{1,0:T(8,128)(2,1)} %reshape.318), kind=kOutput, calls=%fused_computation.5 | convolution fusion | flops 1076363264 | bytes 4194304 | tf_op jit(solution)/shard_map/dot_general | solution.py:95
  181.6 0.8 reshape.319
  182.4 0.0 copy-start.4
  182.4 2.3 %fusion.28 = (bf16[1,512,2,1,128]{4,3,2,1,0:T(2,128)(2,1)S(1)}, bf16[1,512,2,1,128]{4,3,2,1,0:T(2,128)(2,1)}, bf16[1,512,2,1,128]{4,3,2,1,0:T(2,128)(2,1)S(1)}, bf16[1,512,2,1,128]{4,3,2,1,0:T(2,128)(2,1)}) fusion(bf16[1,512,2,4,128]{4,3,2,1,0:T(4,128)(2,1)S(1)} %reshape.319), kind=kLoop, calls=%fused_computation.71 | loop fusion | bytes 2097152 | tf_op jit(solution)/shard_map/slice | solution.py:103
  184.8 1.2 copy.70
  186.0 1.3 multiply_reduce_fusion.3
  187.3 0.0 copy-done.4
  187.3 2.1 multiply_reduce_fusion.2
  189.4 0.0 copy-start.2
  189.4 0.7 copy.71
  190.1 0.1 fusion.8
  190.2 0.2 copy-done.2
  190.4 0.5 convolution_convert_fusion
  190.9 1.1 copy.93
  191.9 3.6 %all-to-all-start.4 = ((bf16[4,512,256]{2,1,0:T(8,128)(2,1)}), bf16[4,512,256]{2,1,0:T(8,128)(2,1)S(1)}, u32[]{:S(2)}, u32[]{:S(2)}) async-start(bf16[4,512,256]{2,1,0:T(8,128)(2,1)} %bitcast.77), calls=%async_computation.4 | async-start | bytes 2097152 | tf_op jit(solution)/shard_map/all_to_all | solution.py:48
  195.5 1.0 constant_dynamic-slice_fusion
  196.5 0.1 copy.72
  196.7 12.4 %all-to-all-done.4 = bf16[4,512,256]{2,1,0:T(8,128)(2,1)S(1)} async-done(((bf16[4,512,256]{2,1,0:T(8,128)(2,1)}), bf16[4,512,256]{2,1,0:T(8,128)(2,1)S(1)}, u32[]{:S(2)}, u32[]{:S(2)}) %all-to-all-start.4) | async-done | bytes 1048608 | tf_op jit(solution)/shard_map/all_to_all | solution.py:48
  209.0 0.1 convert_reduce_fusion
  209.2 0.2 multiply_reduce_fusion.1
  209.5 7.7 %all_to_all.32 = f32[4,1,1024]{2,1,0:T(1,128)S(1)} all-to-all(f32[4,1,1024]{2,1,0:T(1,128)S(1)} %broadcast_in_dim.22), channel_id=1, replica_groups=mesh['grp'=2,'user_0'=32,'user_1'=2,'head'=4] {'head'}, dimensions={0} | all-to-all | bytes 32768 | tf_op jit(solution)/shard_map/all_to_all | solution.py:38
  217.2 0.6 rsqrt_multiply_fusion
  (13 shorter events, 0.2 us)
Async XLA Ops:
  0.0 51.3 %copy-start = (bf16[512,1024]{1,0:T(8,128)(2,1)S(1)}, bf16[512,1024]{1,0:T(8,128)(2,1)}, u32[]{:S(2)}) copy-start(bf16[512,1024]{1,0:T(8,128)(2,1)} %param.11) | copy-start | bytes 3145732
  7.0 66.0 %all-to-all-start = ((s32[32,2,1,16]{3,1,2,0:T(2,128)}), s32[32,2,1,16]{3,1,2,0:T(2,128)S(1)}, u32[]{:S(2)}, u32[]{:S(2)}) async-start(s32[32,2,1,16]{3,1,2,0:T(2,128)} %bitcast.7), calls=%async_computation | async-start | bytes 65536 | tf_op jit(solution)/shard_map/all_to_all | solution.py:27
  83.2 70.9 %all-to-all-start.2 = ((bf16[64,16,256]{2,1,0:T(8,128)(2,1)}), bf16[64,16,256]{2,1,0:T(8,128)(2,1)S(1)}, u32[]{:S(2)}, u32[]{:S(2)}) async-start(bf16[64,16,256]{2,1,0:T(8,128)(2,1)} %bitcast.8), calls=%async_computation.2 | async-start | bytes 1048576 | tf_op jit(solution)/shard_map/all_to_all | solution.py:92
  156.7 6.9 %copy-start.1 = (bf16[1024,2,4,128]{3,2,1,0:T(4,128)(2,1)S(1)}, bf16[1024,2,4,128]{3,2,1,0:T(4,128)(2,1)}, u32[]{:S(2)}) copy-start(bf16[1024,2,4,128]{3,2,1,0:T(4,128)(2,1)} %param.12) | copy-start | bytes 6291460
  159.0 19.1 %all-to-all-start.3 = ((bf16[4,512,256]{1,2,0:T(8,128)(2,1)}), bf16[4,512,256]{1,2,0:T(8,128)(2,1)}, u32[]{:S(2)}, u32[]{:S(2)}) async-start(bf16[4,512,256]{1,2,0:T(8,128)(2,1)} %broadcast_in_dim.20), calls=%async_computation.3 | async-start | bytes 2097152 | tf_op jit(solution)/shard_map/all_to_all | solution.py:38
  163.6 3.4 %copy-start.3 = (bf16[1,512,256]{2,1,0:T(8,128)(2,1)S(1)}, bf16[1,512,256]{2,1,0:T(8,128)(2,1)}, u32[]{:S(2)}) copy-start(bf16[1,512,256]{2,1,0:T(8,128)(2,1)} %param.10) | copy-start | bytes 786436
  182.4 4.9 %copy-start.4 = (bf16[1,512,256]{1,2,0:T(8,128)(2,1)S(1)}, bf16[1,512,256]{1,2,0:T(8,128)(2,1)}, u32[]{:S(2)}) copy-start(bf16[1,512,256]{1,2,0:T(8,128)(2,1)} %copy.65) | copy-start | bytes 786436
  189.4 1.0 copy-start.2
  191.9 17.1 %all-to-all-start.4 = ((bf16[4,512,256]{2,1,0:T(8,128)(2,1)}), bf16[4,512,256]{2,1,0:T(8,128)(2,1)S(1)}, u32[]{:S(2)}, u32[]{:S(2)}) async-start(bf16[4,512,256]{2,1,0:T(8,128)(2,1)} %bitcast.77), calls=%async_computation.4 | async-start | bytes 2097152 | tf_op jit(solution)/shard_map/all_to_all | solution.py:48
where the time goes:
time: 219 us; the launch traced here: 218 us
  waiting for transfers between devices  107 us (49%)
  starting transfers between devices  58.9 us (27%)
  local copies, waits for them, and re-layouts  26.9 us (12%)
  blocking collectives  11.4 us (5%)
  other arithmetic  6.59 us (3%)
  matrix products  5.98 us (3%)
    all_to_all x1, waiting for transfers between devices, body(): lax.all_to_all(looked_up, USER, split_axis=0, concat_axis=0, tiled=True)  64.5 us
    all_to_all x1, starting transfers between devices, moved_by_axis(): lax.all_to_all(pieces, axes[k], split_axis=k, concat_axis=k, tiled=True)  44.3 us
    all_to_all x1, waiting for transfers between devices, moved_by_axis(): lax.all_to_all(pieces, axes[k], split_axis=k, concat_axis=k, tiled=True)  21.6 us
    all_to_all x1, waiting for transfers between devices, sent_and_summed(): lax.all_to_all(pieces, axis, split_axis=0, concat_axis=0, tiled=True)  12.4 us
    all_to_all x1, waiting for transfers between devices, from_everyone(): return lax.all_to_all(copies, axis, split_axis=0, concat_axis=0, tiled=True)  8.61 us
    all_to_all x1, blocking collectives, from_everyone(): return lax.all_to_all(copies, axis, split_axis=0, concat_axis=0, tiled=True)  7.74 us
    all_to_all x1, starting transfers between devices, body(): lax.all_to_all(looked_up, USER, split_axis=0, concat_axis=0, tiled=True)  6.39 us
    gather x1, local copies, waits for them, and re-layouts, body(): looked_up = table_cols[safe_rows].reshape(shard_count, capacity, col_width)  4.95 us
  transfers between devices with their start and end apart: 4, of which 4 were waited for; matrix products, arithmetic and copies ran while one was open for 3% of the time, Pallas kernels for 0%

commit v1 on v0

v1 whole, which is shorter than its diff:
```python
import functools

import jax
import jax.numpy as jnp
from jax import lax
from jax.experimental import pallas as pl
from jax.experimental.pallas import tpu as pltpu
from jax.sharding import PartitionSpec as P

MESH = pl.DeviceIdType.MESH
NT = (((1,), (1,)), ((), ()))
TN = (((0,), (0,)), ((), ()))


def log2(n):
    assert n & (n - 1) == 0
    return n.bit_length() - 1


def silu(v):
    half = 0.5 * v
    return half + half * jnp.tanh(half)


def kernel(
    nz, nh, cap, ids_ref, len_ref, k_hbm, v_hbm, table_hbm, wq_hbm, wo_hbm, out_ref,
    table, wq, keys, values, wfull, req, req_in, rows, emb, gout, gat, slots, part, parts,
    load_sem, req_send, req_recv, row_send, row_recv, fwd_send, fwd_recv, gat_send, gat_recv,
    w_send, w_recv, wp_send, wp_recv, s_send, s_recv,
):
    f32, bf16, i32 = jnp.float32, jnp.bfloat16, jnp.int32
    u, x = lax.axis_index("user"), lax.axis_index("head")
    z, c = u // 2, u % 2
    steps = nz // nh
    n = ids_ref.shape[1]
    shard_rows, d_model = table.shape
    blocks = 2 * nh * steps
    own_class = x + c * (1 - 2 * (x % 2))

    def offset(quarter, j):
        half, odd = j // 2, j % 2
        return quarter + nh * (half + odd * (steps - 1 - 2 * half))

    def shard(j, core):
        quarter = x if core == 0 else x + 1 - 2 * (x % 2)
        return 2 * ((z + offset(quarter, j)) % nz) + core

    def requester(j, core):
        return 2 * ((z + nz - offset(own_class, j)) % nz) + core

    def head(d):
        return (x + d) % nh

    partner = u + 1 - 2 * c

    barrier = pltpu.get_barrier_semaphore()

    def greet(j, carry):
        for core in (0, 1):
            for user in (shard(j, core), requester(j, core)):

                @pl.when(user != u)
                def _():
                    pl.semaphore_signal(
                        barrier, inc=1, device_id={"user": user}, device_id_type=MESH
                    )

        return carry

    lax.fori_loop(0, steps, greet, 0)
    for d in range(1, nh):
        pl.semaphore_signal(barrier, inc=1, device_id={"head": head(d)}, device_id_type=MESH)
    pl.semaphore_signal(barrier, inc=1, device_id={"user": partner}, device_id_type=MESH)

    loads = [
        pltpu.make_async_copy(src, dst, load_sem.at[i])
        for i, (src, dst) in enumerate(
            (
                (table_hbm, table),
                (wq_hbm, wq),
                (k_hbm.at[0], keys),
                (v_hbm.at[0], values),
                (wo_hbm, wfull.at[x]),
            )
        )
    ]
    for load in loads:
        load.start()

    ids = ids_ref[...]
    shard_of = ids >> log2(shard_rows)
    local = ids & (shard_rows - 1)
    core_of = shard_of & 1
    off = ((shard_of >> 1) - z) & (nz - 1)
    turn = off >> log2(nh)
    owner = (off & (nh - 1)) ^ core_of
    step_of = jnp.where(turn < steps // 2, 2 * turn, 2 * (steps - 1 - turn) + 1)
    block_of = (step_of * nh + owner) * 2 + core_of
    in_block = lax.broadcasted_iota(i32, (blocks, n), 0) == block_of
    one_hot = jnp.where(in_block, 1.0, 0.0).astype(bf16)
    before = lax.broadcasted_iota(i32, (n, n), 0) < lax.broadcasted_iota(i32, (n, n), 1)
    earlier = jnp.dot(
        one_hot, jnp.where(before, 1.0, 0.0).astype(bf16), preferred_element_type=f32
    )
    place = jnp.sum(jnp.where(in_block, earlier, 0.0), axis=0, keepdims=True).astype(i32)
    slots[...] = block_of * cap + place
    at_place = (lax.broadcasted_iota(i32, (128, n), 0) & (cap - 1)) == place
    high = jnp.where(at_place, (local >> 5).astype(f32), 0.0).astype(bf16)
    low = jnp.where(at_place, (local & 31).astype(f32), 0.0).astype(bf16)
    wanted = (
        lax.dot_general(one_hot, high, NT, preferred_element_type=f32) * 32.0
        + lax.dot_general(one_hot, low, NT, preferred_element_type=f32)
    ).astype(i32)
    for b in range(blocks):
        req[b] = wanted[b : b + 1]

    others = (own_class + nh - 1) // nh
    pl.semaphore_wait(barrier, 4 * steps + nh - 2 + 2 * others)

    def to_user(src, dst, send_sem, recv_sem, user):
        return pltpu.make_async_remote_copy(
            src_ref=src,
            dst_ref=dst,
            send_sem=send_sem,
            recv_sem=recv_sem,
            device_id={"user": user},
            device_id_type=MESH,
        )

    def to_head(src, dst, send_sem, recv_sem, d):
        return pltpu.make_async_remote_copy(
            src_ref=src,
            dst_ref=dst,
            send_sem=send_sem,
            recv_sem=recv_sem,
            device_id={"head": head(d)},
            device_id_type=MESH,
        )

    def start_unless_self(copy, src, dst, recv_sem, user):
        @pl.when(user != u)
        def _():
            copy.start()

        @pl.when(user == u)
        def _():
            pltpu.make_async_copy(src, dst, recv_sem).start()

    def request(j, core):
        user = shard(j, core)
        src, dst = req.at[(j * nh + x) * 2 + core], req_in.at[j, c]
        return to_user(src, dst, req_send.at[j, core], req_recv.at[j], user), src, dst, user

    def ask(j, carry):
        for core in (0, 1):
            copy, src, dst, user = request(j, core)
            start_unless_self(copy, src, dst, req_recv.at[j], user)
        return carry

    lax.fori_loop(0, steps, ask, 0)

    def half_out(d):
        return to_head(wo_hbm.at[c], wfull.at[x, c], w_send.at[d - 1], w_recv.at[d - 1], d)

    for d in range(1, nh):
        half_out(d).start()

    loads[0].wait()

    def answer(j, core):
        user = requester(j, core)
        src, dst = rows.at[j, core], emb.at[j, x, c]
        return to_user(src, dst, row_send.at[j, core], row_recv.at[j], user), src, dst, user

    def serve(j, carry):
        pltpu.make_async_copy(req_in.at[j], req_in.at[j], req_recv.at[j]).wait()
        lane = lax.broadcasted_iota(i32, (1, 2 * cap), 1)
        both = jnp.where(lane < cap, req_in[j, 0][:, : 2 * cap], req_in[j, 1][:, : 2 * cap])
        pick = lax.broadcasted_iota(i32, (shard_rows, 2 * cap), 0) == both
        found = lax.dot_general(
            jnp.where(pick, 1.0, 0.0).astype(bf16), table[...], TN, preferred_element_type=f32
        )
        rows[j] = found.astype(bf16).reshape(2, cap, d_model)
        for core in (0, 1):
            copy, src, dst, user = answer(j, core)
            start_unless_self(copy, src, dst, row_recv.at[j], user)
        return carry

    lax.fori_loop(0, steps, serve, 0)

    def half_on(d):
        piece = wfull.at[(x + nh - d) % nh, c]
        return to_user(piece, piece, wp_send.at[d - 1], wp_recv.at[d - 1], partner)

    for d in range(1, nh):
        piece = wfull.at[(x + nh - d) % nh, c]
        pltpu.make_async_copy(piece, piece, w_recv.at[d - 1]).wait()
        half_on(d).start()

    for load in loads[1:]:
        load.wait()

    length = len_ref[0, 0]
    head_size = 128
    heads_here = keys.shape[1] // head_size
    prefix = keys.shape[0]
    scale = head_size ** (-0.5)
    per_token = 1.0 / (jnp.zeros((1, 1), f32) + (length + 1).astype(f32))
    inside = lax.broadcasted_iota(i32, (1, prefix), 1) < length
    factor = jnp.where(inside, (0.5 * scale) * per_token, 0.0)

    def forward(j, d):
        mine = emb.at[j, x]
        return to_head(mine, mine, fwd_send.at[j, d - 1], fwd_recv.at[j, d - 1], d)

    def give(j, d):
        return to_head(
            gout.at[j, head(d)], gat.at[j, x], gat_send.at[j, d - 1], gat_recv.at[j, d - 1], d
        )

    def compute(j):
        for d in range(1, nh):
            theirs = emb.at[j, (x + nh - d) % nh]
            pltpu.make_async_copy(theirs, theirs, fwd_recv.at[j, d - 1]).wait()
        embedded = emb[j].reshape(nh * 2 * cap, d_model)
        projected = jnp.dot(embedded, wq[...], preferred_element_type=f32)
        activated = silu(projected).astype(bf16)
        for h in range(heads_here):
            columns = slice(h * head_size, (h + 1) * head_size)
            queries, own_keys, own_values, gates = (
                activated[:, (4 * h + i) * head_size : (4 * h + i + 1) * head_size]
                for i in range(4)
            )
            raw = lax.dot_general(queries, keys[:, columns], NT, preferred_element_type=f32)
            weights = (raw * factor) * (1.0 + jnp.tanh(raw * (0.5 * scale)))
            attended = jnp.dot(
                weights.astype(bf16), values[:, columns], preferred_element_type=f32
            )
            own_dot = jnp.sum(
                queries.astype(f32) * own_keys.astype(f32), axis=1, keepdims=True
            )
            own_weight = silu(own_dot * scale) * per_token
            attended = attended + own_weight * own_values.astype(f32)
            mean_square = jnp.mean(attended * attended, axis=1, keepdims=True)
            gated = attended * lax.rsqrt(mean_square + 1e-06) * gates.astype(f32)
            gout[j, :, :, columns] = gated.astype(bf16).reshape(nh, 2 * cap, head_size)
        for d in range(1, nh):
            give(j, d).start()

    def stage(j, carry):
        @pl.when(j < steps)
        def _():
            mine = emb.at[j, x]
            pltpu.make_async_copy(mine, mine, row_recv.at[j]).wait()
            for d in range(1, nh):
                forward(j, d).start()

        @pl.when(j >= 1)
        def _():
            compute(j - 1)

        return carry

    lax.fori_loop(0, steps + 1, stage, 0)

    for d in range(1, nh):
        piece = wfull.at[(x + nh - d) % nh, 1 - c]
        pltpu.make_async_copy(piece, piece, wp_recv.at[d - 1]).wait()

    def collect(j, carry):
        for d in range(1, nh):
            theirs = gat.at[j, (x + nh - d) % nh]
            pltpu.make_async_copy(theirs, theirs, gat_recv.at[j, d - 1]).wait()
        gat[j, x] = gout[j, x]
        return carry

    lax.fori_loop(0, steps, collect, 0)
    own = steps * 2 * cap
    width = gat.shape[-1]
    summed = jnp.zeros((own, d_model), f32)
    for y in range(nh):
        summed = summed + jnp.dot(
            gat[:, y].reshape(own, width),
            wfull[y].reshape(width, d_model),
            preferred_element_type=f32,
        )
    mine = emb[:, pl.ds(x, 1)].reshape(own, d_model).astype(f32)
    inner = jnp.sum(summed * mine, axis=1, keepdims=True)
    square = jnp.sum(summed * summed, axis=1, keepdims=True)
    score = inner * d_model ** (-0.5) * lax.rsqrt(square / d_model + 1e-06)
    row = lax.broadcasted_iota(i32, (own, n), 0)
    slot = ((row >> log2(2 * cap)) * nh + x) * (2 * cap) + (row & (2 * cap - 1))
    part[...] = jnp.sum(jnp.where(slot == slots[...], score, 0.0), axis=0, keepdims=True)

    def share(d):
        return to_head(part, parts.at[d - 1], s_send.at[d - 1], s_recv.at[d - 1], d)

    for d in range(1, nh):
        share(d).start()
    total = part[...]
    for d in range(1, nh):
        pltpu.make_async_copy(parts.at[d - 1], parts.at[d - 1], s_recv.at[d - 1]).wait()
        total = total + parts[d - 1]
    out_ref[...] = total

    def drain(j, carry):
        for core in (0, 1):
            for make in (request, answer):
                copy, _, _, user = make(j, core)

                @pl.when(user != u)
                def _():
                    copy.wait_send()

        for d in range(1, nh):
            forward(j, d).wait_send()
            give(j, d).wait_send()
        return carry

    lax.fori_loop(0, steps, drain, 0)
    for d in range(1, nh):
        half_out(d).wait_send()
        half_on(d).wait_send()
        share(d).wait_send()


def body(nz, nh, cand_ids, prefix_len, key_cache, value_cache, item_table, w_qkvu, w_out):
    n = cand_ids.shape[1]
    prefix, width = key_cache.shape[1:]
    shard_rows, d_model = item_table.shape
    steps = nz // nh
    blocks = 2 * nz
    cap = 2 * n // blocks
    bf16, dma = jnp.bfloat16, pltpu.SemaphoreType.DMA
    vmem = pl.BlockSpec(memory_space=pltpu.VMEM)
    hbm = pl.BlockSpec(memory_space=pl.ANY)
    wq = w_qkvu.reshape(d_model, -1)
    return pl.pallas_call(
        functools.partial(kernel, nz, nh, cap),
        out_shape=jax.ShapeDtypeStruct((1, n), jnp.float32),
        in_specs=[vmem, pl.BlockSpec(memory_space=pltpu.SMEM)] + [hbm] * 5,
        out_specs=vmem,
        scratch_shapes=[
            pltpu.VMEM((shard_rows, d_model), bf16),
            pltpu.VMEM(wq.shape, bf16),
            pltpu.VMEM((prefix, width), bf16),
            pltpu.VMEM((prefix, width), bf16),
            pltpu.VMEM((nh, *w_out.shape), bf16),
            pltpu.VMEM((blocks, 1, 128), jnp.int32),
            pltpu.VMEM((steps, 2, 1, 128), jnp.int32),
            pltpu.VMEM((steps, 2, cap, d_model), bf16),
            pltpu.VMEM((steps, nh, 2, cap, d_model), bf16),
            pltpu.VMEM((steps, nh, 2 * cap, width), bf16),
            pltpu.VMEM((steps, nh, 2 * cap, width), bf16),
            pltpu.VMEM((1, n), jnp.int32),
            pltpu.VMEM((1, n), jnp.float32),
            pltpu.VMEM((nh - 1, 1, n), jnp.float32),
            dma((5,)),
            dma((steps, 2)),
            dma((steps,)),
            dma((steps, 2)),
            dma((steps,)),
            dma((steps, nh - 1)),
            dma((steps, nh - 1)),
            dma((steps, nh - 1)),
            dma((steps, nh - 1)),
            dma((nh - 1,)),
            dma((nh - 1,)),
            dma((nh - 1,)),
            dma((nh - 1,)),
            dma((nh - 1,)),
            dma((nh - 1,)),
        ],
        compiler_params=pltpu.CompilerParams(
            collective_id=0, has_side_effects=True, vmem_limit_bytes=48 * 1024 * 1024
        ),
    )(cand_ids, prefix_len.reshape(1, 1), key_cache, value_cache, item_table, wq, w_out)


def solution(mesh):
    users = ("grp", "user")
    return jax.shard_map(
        functools.partial(body, mesh.shape["user"] // 2, mesh.shape["head"]),
        mesh=mesh,
        in_specs=(
            P(users, None),
            P(users),
            P(users, None, "head"),
            P(users, None, "head"),
            P("user", None),
            P(None, "head", None, None),
            P("head", None, None),
        ),
        out_specs=P(users, None),
        check_vma=False,
    )
```

time: 219 us -> 133 us (0.61)
  the two profiles are of different devices: /device:TPU:104 before, /device:TPU:160 now
where the time goes in v1:
time: 133 us
  Pallas kernels  126 us (95%)
  local copies, waits for them, and re-layouts  5.91 us (4%)
    pallas_call x1, Pallas kernels, body(): pl.pallas_call(functools.partial(kernel, nz, nh, cap), out_shape=jax.Shap...  126 us
    reshape x1, local copies, waits for them, and re-layouts, body(): wq = w_qkvu.reshape(d_model, -1)  3.33 us

profile of v1, /device:TPU:160, one launch (start us, length us, event | category | flops | bytes accessed | tf_op | source)
XLA Modules:
  0.0 132.7 jit_solution(3338606729267332841)
XLA Ops:
  0.7 0.0 copy-start
  0.7 0.0 copy-start.2
  0.7 0.0 copy-start.4
  0.7 3.3 %reshape.7.wq_hbm = bf16[1024,1024]{1,0:T(8,128)(2,1)S(1)} reshape(bf16[1024,2,4,128]{3,2,1,0:T(4,128)(2,1)} %param.12) | data formatting | bytes 4194304 | tf_op jit(solution)/shard_map/reshape | solution.py:337
  4.0 0.0 copy-done
  4.0 0.0 copy-done.2
  4.0 0.0 copy-done.4
  4.1 0.0 copy-start.1
  4.1 1.0 copy-done.1
  5.1 0.0 copy-start.3
  5.1 0.9 copy-done.3
  6.0 126.1 %shard_map.73 = f32[1,512]{1,0:T(1,128)S(1)} custom-call(s32[1,512]{1,0:T(1,128)S(1)} %copy-done.4, s32[1,1]{1,0:T(1,128)} %bitcast.1.len_ref, bf16[1,512,256]{2,1,0:T(8,128)(2,1)S(1)} %copy-done.2, bf16[1,512,256]{2,1,0:T(8,128)(2,1)S(1)} %copy-done.3, bf16[512,1024]{1,0:T(8,128)(2,1)S(1)} %copy-done, bf16[1024,1024]{1,0:T(8,128)(2,1)S(1)} %reshape.7.wq_hbm, ...), custom_call_target="tpu_custom_call" | custom-call | tf_op jit(solution)/shard_map/pallas_call | solution.py:338
  132.1 0.6 copy.10
Async XLA Ops:
  0.7 3.4 %copy-start = (bf16[512,1024]{1,0:T(8,128)(2,1)S(1)}, bf16[512,1024]{1,0:T(8,128)(2,1)}, u32[]{:S(2)}) copy-start(bf16[512,1024]{1,0:T(8,128)(2,1)} %table_hbm.1) | copy-start | bytes 3145732
  0.7 3.4 %copy-start.2 = (bf16[1,512,256]{2,1,0:T(8,128)(2,1)S(1)}, bf16[1,512,256]{2,1,0:T(8,128)(2,1)}, u32[]{:S(2)}) copy-start(bf16[1,512,256]{2,1,0:T(8,128)(2,1)} %k_hbm.1) | copy-start | bytes 786436
  0.7 3.4 %copy-start.4 = (s32[1,512]{1,0:T(1,128)S(1)}, s32[1,512]{1,0:T(1,128)}, u32[]{:S(2)}) copy-start(s32[1,512]{1,0:T(1,128)} %ids_ref.1) | copy-start | bytes 6148
  4.1 1.0 copy-start.1
  5.1 0.9 copy-start.3

commit v2 on v1

--- a/solution.py
+++ b/solution.py
@@ -24,7 +24,7 @@
 
 def kernel(
     nz, nh, cap, ids_ref, len_ref, k_hbm, v_hbm, table_hbm, wq_hbm, wo_hbm, out_ref,
-    table, wq, keys, values, wfull, req, req_in, rows, emb, gout, gat, slots, part, parts,
+    table, wq_in, wq, keys, values, wfull, req, req_in, rows, emb, gout, gat, slots, part, parts,
     load_sem, req_send, req_recv, row_send, row_recv, fwd_send, fwd_recv, gat_send, gat_recv,
     w_send, w_recv, wp_send, wp_recv, s_send, s_recv,
 ):
@@ -77,7 +77,7 @@
         for i, (src, dst) in enumerate(
             (
                 (table_hbm, table),
-                (wq_hbm, wq),
+                (wq_hbm, wq_in),
                 (k_hbm.at[0], keys),
                 (v_hbm.at[0], values),
                 (wo_hbm, wfull.at[x]),
@@ -115,6 +115,17 @@
         req[b] = wanted[b : b + 1]
 
     others = (own_class + nh - 1) // nh
+    for load in loads[1:]:
+        load.wait()
+    span = 128
+
+    def relay_weights(i, carry):
+        at = pl.ds(pl.multiple_of(i * span, span), span)
+        wq[at, :] = wq_in[at].reshape(span, wq.shape[1])
+        return carry
+
+    lax.fori_loop(0, d_model // span, relay_weights, 0)
+
     pl.semaphore_wait(barrier, 4 * steps + nh - 2 + 2 * others)
 
     def to_user(src, dst, send_sem, recv_sem, user):
@@ -196,9 +207,6 @@
         piece = wfull.at[(x + nh - d) % nh, c]
         pltpu.make_async_copy(piece, piece, w_recv.at[d - 1]).wait()
         half_on(d).start()
-
-    for load in loads[1:]:
-        load.wait()
 
     length = len_ref[0, 0]
     head_size = 128
@@ -334,7 +342,7 @@
     bf16, dma = jnp.bfloat16, pltpu.SemaphoreType.DMA
     vmem = pl.BlockSpec(memory_space=pltpu.VMEM)
     hbm = pl.BlockSpec(memory_space=pl.ANY)
-    wq = w_qkvu.reshape(d_model, -1)
+    wq_width = w_qkvu.size // d_model
     return pl.pallas_call(
         functools.partial(kernel, nz, nh, cap),
         out_shape=jax.ShapeDtypeStruct((1, n), jnp.float32),
@@ -342,7 +350,8 @@
         out_specs=vmem,
         scratch_shapes=[
             pltpu.VMEM((shard_rows, d_model), bf16),
-            pltpu.VMEM(wq.shape, bf16),
+            pltpu.VMEM(w_qkvu.shape, bf16),
+            pltpu.VMEM((d_model, wq_width), bf16),
             pltpu.VMEM((prefix, width), bf16),
             pltpu.VMEM((prefix, width), bf16),
             pltpu.VMEM((nh, *w_out.shape), bf16),
@@ -372,9 +381,9 @@
             dma((nh - 1,)),
         ],
         compiler_params=pltpu.CompilerParams(
-            collective_id=0, has_side_effects=True, vmem_limit_bytes=48 * 1024 * 1024
+            collective_id=0, has_side_effects=True, vmem_limit_bytes=67_043_328
         ),
-    )(cand_ids, prefix_len.reshape(1, 1), key_cache, value_cache, item_table, wq, w_out)
+    )(cand_ids, prefix_len.reshape(1, 1), key_cache, value_cache, item_table, w_qkvu, w_out)
 
 
 def solution(mesh):

time: 133 us -> 130 us (0.977)
  the two profiles are of different devices: /device:TPU:160 before, /device:TPU:105 now
where the time goes in v2:
time: 130 us
  Pallas kernels  128 us (98%)
    pallas_call x1, Pallas kernels, body(): pl.pallas_call(functools.partial(kernel, nz, nh, cap), out_shape=jax.Shap...  128 us

profile of v2, /device:TPU:105, one launch (start us, length us, event | category | flops | bytes accessed | tf_op | source)
XLA Modules:
  0.0 130.1 jit_solution(6305938591872514323)
XLA Ops:
  0.7 128.2 %shard_map.73 = f32[1,512]{1,0:T(1,128)} custom-call(s32[1,512]{1,0:T(1,128)} %ids_ref.1, s32[1,1]{1,0:T(1,128)} %bitcast.1.len_ref, bf16[1,512,256]{2,1,0:T(8,128)(2,1)} %k_hbm.1, bf16[1,512,256]{2,1,0:T(8,128)(2,1)} %v_hbm.1, bf16[512,1024]{1,0:T(8,128)(2,1)} %table_hbm.1, bf16[1024,2,4,128]{3,2,1,0:T(4,128)(2,1)} %wq_hbm.1, bf16[2,128,1024]{2,1,0:T(8,128)(2,1)} %wo_hbm.1), custom_call_target="tpu_custom_call" | custom-call | tf_op jit(solution)/shard_map/pallas_call | solution.py:346
  128.9 1.3 copy.10

commit v3 on v2

--- a/solution.py
+++ b/solution.py
@@ -8,6 +8,7 @@
 from jax.sharding import PartitionSpec as P
 
 MESH = pl.DeviceIdType.MESH
+LAG = 2
 NT = (((1,), (1,)), ((), ()))
 TN = (((0,), (0,)), ((), ()))
 
@@ -23,8 +24,8 @@
 
 
 def kernel(
-    nz, nh, cap, ids_ref, len_ref, k_hbm, v_hbm, table_hbm, wq_hbm, wo_hbm, out_ref,
-    table, wq_in, wq, keys, values, wfull, req, req_in, rows, emb, gout, gat, slots, part, parts,
+    nz, nh, cap, ids_hbm, len_hbm, k_hbm, v_hbm, table_hbm, wq_hbm, wo_hbm, out_ref,
+    ids_ref, len_ref, table, wq_in, wq, keys, values, wfull, req, req_in, rows, emb, gout, gat, slots, part,
     load_sem, req_send, req_recv, row_send, row_recv, fwd_send, fwd_recv, gat_send, gat_recv,
     w_send, w_recv, wp_send, wp_recv, s_send, s_recv,
 ):
@@ -32,17 +33,17 @@
     u, x = lax.axis_index("user"), lax.axis_index("head")
     z, c = u // 2, u % 2
     steps = nz // nh
-    n = ids_ref.shape[1]
+    n = ids_hbm.shape[1]
     shard_rows, d_model = table.shape
     blocks = 2 * nh * steps
-    own_class = x + c * (1 - 2 * (x % 2))
+    own_class = (x + c * (nh // 2)) % nh
 
     def offset(quarter, j):
         half, odd = j // 2, j % 2
         return quarter + nh * (half + odd * (steps - 1 - 2 * half))
 
     def shard(j, core):
-        quarter = x if core == 0 else x + 1 - 2 * (x % 2)
+        quarter = (x + core * (nh // 2)) % nh
         return 2 * ((z + offset(quarter, j)) % nz) + core
 
     def requester(j, core):
@@ -55,7 +56,8 @@
 
     barrier = pltpu.get_barrier_semaphore()
 
-    def greet(j, carry):
+    def greet(i, carry):
+        j = steps - 1 - i
         for core in (0, 1):
             for user in (shard(j, core), requester(j, core)):
 
@@ -81,11 +83,14 @@
                 (k_hbm.at[0], keys),
                 (v_hbm.at[0], values),
                 (wo_hbm, wfull.at[x]),
+                (ids_hbm, ids_ref),
+                (len_hbm, len_ref),
             )
         )
     ]
-    for load in loads:
+    for load in loads[5:] + loads[:5]:
         load.start()
+    loads[5].wait()
 
     ids = ids_ref[...]
     shard_of = ids >> log2(shard_rows)
@@ -93,7 +98,7 @@
     core_of = shard_of & 1
     off = ((shard_of >> 1) - z) & (nz - 1)
     turn = off >> log2(nh)
-    owner = (off & (nh - 1)) ^ core_of
+    owner = (off - core_of * (nh // 2)) & (nh - 1)
     step_of = jnp.where(turn < steps // 2, 2 * turn, 2 * (steps - 1 - turn) + 1)
     block_of = (step_of * nh + owner) * 2 + core_of
     in_block = lax.broadcasted_iota(i32, (blocks, n), 0) == block_of
@@ -115,18 +120,8 @@
         req[b] = wanted[b : b + 1]
 
     others = (own_class + nh - 1) // nh
-    for load in loads[1:]:
-        load.wait()
-    span = 128
-
-    def relay_weights(i, carry):
-        at = pl.ds(pl.multiple_of(i * span, span), span)
-        wq[at, :] = wq_in[at].reshape(span, wq.shape[1])
-        return carry
-
-    lax.fori_loop(0, d_model // span, relay_weights, 0)
-
-    pl.semaphore_wait(barrier, 4 * steps + nh - 2 + 2 * others)
+    with jax.named_scope("barrier"):
+        pl.semaphore_wait(barrier, 4 * steps + nh - 2 + 2 * others)
 
     def to_user(src, dst, send_sem, recv_sem, user):
         return pltpu.make_async_remote_copy(
@@ -162,13 +157,15 @@
         src, dst = req.at[(j * nh + x) * 2 + core], req_in.at[j, c]
         return to_user(src, dst, req_send.at[j, core], req_recv.at[j], user), src, dst, user
 
-    def ask(j, carry):
+    def ask(i, carry):
+        j = steps - 1 - i
         for core in (0, 1):
             copy, src, dst, user = request(j, core)
             start_unless_self(copy, src, dst, req_recv.at[j], user)
         return carry
 
-    lax.fori_loop(0, steps, ask, 0)
+    with jax.named_scope("ask"):
+        lax.fori_loop(0, steps, ask, 0)
 
     def half_out(d):
         return to_head(wo_hbm.at[c], wfull.at[x, c], w_send.at[d - 1], w_recv.at[d - 1], d)
@@ -184,7 +181,8 @@
         return to_user(src, dst, row_send.at[j, core], row_recv.at[j], user), src, dst, user
 
     def serve(j, carry):
-        pltpu.make_async_copy(req_in.at[j], req_in.at[j], req_recv.at[j]).wait()
+        with jax.named_scope("req_wait"):
+            pltpu.make_async_copy(req_in.at[j], req_in.at[j], req_recv.at[j]).wait()
         lane = lax.broadcasted_iota(i32, (1, 2 * cap), 1)
         both = jnp.where(lane < cap, req_in[j, 0][:, : 2 * cap], req_in[j, 1][:, : 2 * cap])
         pick = lax.broadcasted_iota(i32, (shard_rows, 2 * cap), 0) == both
@@ -205,8 +203,21 @@
 
     for d in range(1, nh):
         piece = wfull.at[(x + nh - d) % nh, c]
-        pltpu.make_async_copy(piece, piece, w_recv.at[d - 1]).wait()
+        with jax.named_scope("w_wait"):
+            pltpu.make_async_copy(piece, piece, w_recv.at[d - 1]).wait()
         half_on(d).start()
+
+    for load in loads[1:5] + loads[6:]:
+        load.wait()
+    span = 128
+
+    def relay_weights(i, carry):
+        at = pl.ds(pl.multiple_of(i * span, span), span)
+        wq[at, :] = wq_in[at].reshape(span, wq.shape[1])
+        return carry
+
+    with jax.named_scope("relay"):
+        lax.fori_loop(0, d_model // span, relay_weights, 0)
 
     length = len_ref[0, 0]
     head_size = 128
@@ -229,7 +240,8 @@
     def compute(j):
         for d in range(1, nh):
             theirs = emb.at[j, (x + nh - d) % nh]
-            pltpu.make_async_copy(theirs, theirs, fwd_recv.at[j, d - 1]).wait()
+            with jax.named_scope("fwd_wait"):
+                pltpu.make_async_copy(theirs, theirs, fwd_recv.at[j, d - 1]).wait()
         embedded = emb[j].reshape(nh * 2 * cap, d_model)
         projected = jnp.dot(embedded, wq[...], preferred_element_type=f32)
         activated = silu(projected).astype(bf16)
@@ -259,26 +271,29 @@
         @pl.when(j < steps)
         def _():
             mine = emb.at[j, x]
-            pltpu.make_async_copy(mine, mine, row_recv.at[j]).wait()
+            with jax.named_scope("row_wait"):
+                pltpu.make_async_copy(mine, mine, row_recv.at[j]).wait()
             for d in range(1, nh):
                 forward(j, d).start()
 
-        @pl.when(j >= 1)
+        @pl.when(j >= LAG)
         def _():
-            compute(j - 1)
-
-        return carry
-
-    lax.fori_loop(0, steps + 1, stage, 0)
+            compute(j - LAG)
+
+        return carry
+
+    lax.fori_loop(0, steps + LAG, stage, 0)
 
     for d in range(1, nh):
         piece = wfull.at[(x + nh - d) % nh, 1 - c]
-        pltpu.make_async_copy(piece, piece, wp_recv.at[d - 1]).wait()
+        with jax.named_scope("wp_wait"):
+            pltpu.make_async_copy(piece, piece, wp_recv.at[d - 1]).wait()
 
     def collect(j, carry):
         for d in range(1, nh):
             theirs = gat.at[j, (x + nh - d) % nh]
-            pltpu.make_async_copy(theirs, theirs, gat_recv.at[j, d - 1]).wait()
+            with jax.named_scope("gat_wait"):
+                pltpu.make_async_copy(theirs, theirs, gat_recv.at[j, d - 1]).wait()
         gat[j, x] = gout[j, x]
         return carry
 
@@ -301,15 +316,12 @@
     part[...] = jnp.sum(jnp.where(slot == slots[...], score, 0.0), axis=0, keepdims=True)
 
     def share(d):
-        return to_head(part, parts.at[d - 1], s_send.at[d - 1], s_recv.at[d - 1], d)
+        return to_head(part, out_ref.at[x], s_send.at[d - 1], s_recv.at[d - 1], d)
 
     for d in range(1, nh):
         share(d).start()
-    total = part[...]
-    for d in range(1, nh):
-        pltpu.make_async_copy(parts.at[d - 1], parts.at[d - 1], s_recv.at[d - 1]).wait()
-        total = total + parts[d - 1]
-    out_ref[...] = total
+    keep = pltpu.make_async_copy(part, out_ref.at[x], load_sem.at[0])
+    keep.start()
 
     def drain(j, carry):
         for core in (0, 1):
@@ -325,11 +337,17 @@
             give(j, d).wait_send()
         return carry
 
-    lax.fori_loop(0, steps, drain, 0)
+    with jax.named_scope("drain"):
+        lax.fori_loop(0, steps, drain, 0)
     for d in range(1, nh):
         half_out(d).wait_send()
         half_on(d).wait_send()
+    keep.wait()
+    for d in range(1, nh):
         share(d).wait_send()
+        theirs = out_ref.at[(x + nh - d) % nh]
+        with jax.named_scope("s_wait"):
+            pltpu.make_async_copy(theirs, theirs, s_recv.at[d - 1]).wait()
 
 
 def body(nz, nh, cand_ids, prefix_len, key_cache, value_cache, item_table, w_qkvu, w_out):
@@ -340,15 +358,16 @@
     blocks = 2 * nz
     cap = 2 * n // blocks
     bf16, dma = jnp.bfloat16, pltpu.SemaphoreType.DMA
-    vmem = pl.BlockSpec(memory_space=pltpu.VMEM)
     hbm = pl.BlockSpec(memory_space=pl.ANY)
     wq_width = w_qkvu.size // d_model
-    return pl.pallas_call(
+    parts = pl.pallas_call(
         functools.partial(kernel, nz, nh, cap),
-        out_shape=jax.ShapeDtypeStruct((1, n), jnp.float32),
-        in_specs=[vmem, pl.BlockSpec(memory_space=pltpu.SMEM)] + [hbm] * 5,
-        out_specs=vmem,
+        out_shape=jax.ShapeDtypeStruct((nh, 1, n), jnp.float32),
+        in_specs=[hbm] * 7,
+        out_specs=hbm,
         scratch_shapes=[
+            pltpu.VMEM((1, n), jnp.int32),
+            pltpu.SMEM((1, 1), jnp.int32),
             pltpu.VMEM((shard_rows, d_model), bf16),
             pltpu.VMEM(w_qkvu.shape, bf16),
             pltpu.VMEM((d_model, wq_width), bf16),
@@ -363,8 +382,7 @@
             pltpu.VMEM((steps, nh, 2 * cap, width), bf16),
             pltpu.VMEM((1, n), jnp.int32),
             pltpu.VMEM((1, n), jnp.float32),
-            pltpu.VMEM((nh - 1, 1, n), jnp.float32),
-            dma((5,)),
+            dma((7,)),
             dma((steps, 2)),
             dma((steps,)),
             dma((steps, 2)),
@@ -384,6 +402,7 @@
             collective_id=0, has_side_effects=True, vmem_limit_bytes=67_043_328
         ),
     )(cand_ids, prefix_len.reshape(1, 1), key_cache, value_cache, item_table, w_qkvu, w_out)
+    return jnp.sum(parts, axis=0)
 
 
 def solution(mesh):

time: 130 us -> 128 us (0.985)
  the two profiles are of different devices: /device:TPU:105 before, /device:TPU:40 now
where the time goes in v3:
time: 128 us; the launch traced here: 127 us
  Pallas kernels  125 us (98%)
  other arithmetic  1.3 us (1%)
    pallas_call x1, Pallas kernels, body(): pl.pallas_call(functools.partial(kernel, nz, nh, cap), out_shape=jax.Shap...  125 us

profile of v3, /device:TPU:40, one launch (start us, length us, event | category | flops | bytes accessed | tf_op | source)
XLA Modules:
  0.0 127.4 jit_solution(9923393273995528490)
XLA Ops:
  0.7 125.5 %shard_map.73 = f32[4,1,512]{2,1,0:T(1,128)} custom-call(s32[1,512]{1,0:T(1,128)} %ids_hbm.1, s32[1,1]{1,0:T(1,128)} %bitcast.2.len_hbm, bf16[1,512,256]{2,1,0:T(8,128)(2,1)} %k_hbm.1, bf16[1,512,256]{2,1,0:T(8,128)(2,1)} %v_hbm.1, bf16[512,1024]{1,0:T(8,128)(2,1)} %table_hbm.1, bf16[1024,2,4,128]{3,2,1,0:T(4,128)(2,1)} %wq_hbm.1, bf16[2,128,1024]{2,1,0:T(8,128)(2,1)} %wo_hbm.1), custom_call_target="tpu_custom_call" | custom-call | tf_op jit(solution)/shard_map/pallas_call | solution.py:363
  126.1 1.3 %reduce_sum.11 = f32[512]{0:T(512)} reduce(f32[4,1,512]{2,1,0:T(1,128)} %shard_map.73, f32[]{:T(128)} %constant.0.clone.1), dimensions={0,1}, to_apply=%region_0.0 | reduce | flops 1536 | bytes 10244 | tf_op jit(solution)/shard_map/reduce_sum | solution.py:405

commit v4 on v3

--- a/solution.py
+++ b/solution.py
@@ -39,8 +39,9 @@
     own_class = (x + c * (nh // 2)) % nh
 
     def offset(quarter, j):
-        half, odd = j // 2, j % 2
-        return quarter + nh * (half + odd * (steps - 1 - 2 * half))
+        flip = quarter // (nh // 2 + 1)
+        half, back = j // 2, (j + flip) % 2
+        return quarter + nh * (half + back * (steps - 1 - 2 * half))
 
     def shard(j, core):
         quarter = (x + core * (nh // 2)) % nh
@@ -56,8 +57,7 @@
 
     barrier = pltpu.get_barrier_semaphore()
 
-    def greet(i, carry):
-        j = steps - 1 - i
+    def greet(j, carry):
         for core in (0, 1):
             for user in (shard(j, core), requester(j, core)):
 
@@ -98,8 +98,12 @@
     core_of = shard_of & 1
     off = ((shard_of >> 1) - z) & (nz - 1)
     turn = off >> log2(nh)
-    owner = (off - core_of * (nh // 2)) & (nh - 1)
-    step_of = jnp.where(turn < steps // 2, 2 * turn, 2 * (steps - 1 - turn) + 1)
+    quarter_of = off & (nh - 1)
+    owner = (quarter_of - core_of * (nh // 2)) & (nh - 1)
+    flip_of = jnp.where(quarter_of > nh // 2, 1, 0)
+    step_of = jnp.where(
+        turn < steps // 2, 2 * turn + flip_of, 2 * (steps - 1 - turn) + 1 - flip_of
+    )
     block_of = (step_of * nh + owner) * 2 + core_of
     in_block = lax.broadcasted_iota(i32, (blocks, n), 0) == block_of
     one_hot = jnp.where(in_block, 1.0, 0.0).astype(bf16)
@@ -157,8 +161,7 @@
         src, dst = req.at[(j * nh + x) * 2 + core], req_in.at[j, c]
         return to_user(src, dst, req_send.at[j, core], req_recv.at[j], user), src, dst, user
 
-    def ask(i, carry):
-        j = steps - 1 - i
+    def ask(j, carry):
         for core in (0, 1):
             copy, src, dst, user = request(j, core)
             start_unless_self(copy, src, dst, req_recv.at[j], user)

time: 128 us -> 125 us (0.977)
  the two profiles are of different devices: /device:TPU:40 before, /device:TPU:97 now
where the time goes in v4:
time: 125 us
  Pallas kernels  123 us (98%)
  other arithmetic  1.3 us (1%)
    pallas_call x1, Pallas kernels, body(): pl.pallas_call(functools.partial(kernel, nz, nh, cap), out_shape=jax.Shap...  123 us

profile of v4, /device:TPU:97, one launch (start us, length us, event | category | flops | bytes accessed | tf_op | source)
XLA Modules:
  0.0 125.3 jit_solution(9067266318496234411)
XLA Ops:
  0.7 123.3 %shard_map.73 = f32[4,1,512]{2,1,0:T(1,128)} custom-call(s32[1,512]{1,0:T(1,128)} %ids_hbm.1, s32[1,1]{1,0:T(1,128)} %bitcast.2.len_hbm, bf16[1,512,256]{2,1,0:T(8,128)(2,1)} %k_hbm.1, bf16[1,512,256]{2,1,0:T(8,128)(2,1)} %v_hbm.1, bf16[512,1024]{1,0:T(8,128)(2,1)} %table_hbm.1, bf16[1024,2,4,128]{3,2,1,0:T(4,128)(2,1)} %wq_hbm.1, bf16[2,128,1024]{2,1,0:T(8,128)(2,1)} %wo_hbm.1), custom_call_target="tpu_custom_call" | custom-call | tf_op jit(solution)/shard_map/pallas_call | solution.py:366
  124.0 1.3 %reduce_sum.11 = f32[512]{0:T(512)} reduce(f32[4,1,512]{2,1,0:T(1,128)} %shard_map.73, f32[]{:T(128)} %constant.0.clone.1), dimensions={0,1}, to_apply=%region_0.0 | reduce | flops 1536 | bytes 10244 | tf_op jit(solution)/shard_map/reduce_sum | solution.py:408

commit v5 on v4

--- a/solution.py
+++ b/solution.py
@@ -54,6 +54,7 @@
         return (x + d) % nh
 
     partner = u + 1 - 2 * c
+    farthest_first = sorted(range(1, nh), key=lambda d: -min(d, nh - d))
 
     barrier = pltpu.get_barrier_semaphore()
 
@@ -222,7 +223,7 @@
     with jax.named_scope("relay"):
         lax.fori_loop(0, d_model // span, relay_weights, 0)
 
-    length = len_ref[0, 0]
+    length = len_ref[0]
     head_size = 128
     heads_here = keys.shape[1] // head_size
     prefix = keys.shape[0]
@@ -267,7 +268,7 @@
             mean_square = jnp.mean(attended * attended, axis=1, keepdims=True)
             gated = attended * lax.rsqrt(mean_square + 1e-06) * gates.astype(f32)
             gout[j, :, :, columns] = gated.astype(bf16).reshape(nh, 2 * cap, head_size)
-        for d in range(1, nh):
+        for d in farthest_first:
             give(j, d).start()
 
     def stage(j, carry):
@@ -276,7 +277,7 @@
             mine = emb.at[j, x]
             with jax.named_scope("row_wait"):
                 pltpu.make_async_copy(mine, mine, row_recv.at[j]).wait()
-            for d in range(1, nh):
+            for d in farthest_first:
                 forward(j, d).start()
 
         @pl.when(j >= LAG)
@@ -300,28 +301,32 @@
         gat[j, x] = gout[j, x]
         return carry
 
-    lax.fori_loop(0, steps, collect, 0)
-    own = steps * 2 * cap
-    width = gat.shape[-1]
-    summed = jnp.zeros((own, d_model), f32)
-    for y in range(nh):
-        summed = summed + jnp.dot(
-            gat[:, y].reshape(own, width),
-            wfull[y].reshape(width, d_model),
-            preferred_element_type=f32,
-        )
-    mine = emb[:, pl.ds(x, 1)].reshape(own, d_model).astype(f32)
-    inner = jnp.sum(summed * mine, axis=1, keepdims=True)
-    square = jnp.sum(summed * summed, axis=1, keepdims=True)
-    score = inner * d_model ** (-0.5) * lax.rsqrt(square / d_model + 1e-06)
-    row = lax.broadcasted_iota(i32, (own, n), 0)
-    slot = ((row >> log2(2 * cap)) * nh + x) * (2 * cap) + (row & (2 * cap - 1))
-    part[...] = jnp.sum(jnp.where(slot == slots[...], score, 0.0), axis=0, keepdims=True)
+    def scored(first, count):
+        own, width = count * 2 * cap, gat.shape[-1]
+        summed = jnp.zeros((own, d_model), f32)
+        for y in range(nh):
+            summed = summed + jnp.dot(
+                gat[first : first + count, y].reshape(own, width),
+                wfull[y].reshape(width, d_model),
+                preferred_element_type=f32,
+            )
+        mine = emb[first : first + count, pl.ds(x, 1)].reshape(own, d_model).astype(f32)
+        inner = jnp.sum(summed * mine, axis=1, keepdims=True)
+        square = jnp.sum(summed * summed, axis=1, keepdims=True)
+        score = inner * d_model ** (-0.5) * lax.rsqrt(square / d_model + 1e-06)
+        row = lax.broadcasted_iota(i32, (own, n), 0)
+        slot = ((first + (row >> log2(2 * cap))) * nh + x) * (2 * cap) + (row & (2 * cap - 1))
+        return jnp.sum(jnp.where(slot == slots[...], score, 0.0), axis=0, keepdims=True)
+
+    lax.fori_loop(0, steps - 1, collect, 0)
+    part[...] = scored(0, steps - 1)
+    collect(steps - 1, 0)
+    part[...] += scored(steps - 1, 1)
 
     def share(d):
         return to_head(part, out_ref.at[x], s_send.at[d - 1], s_recv.at[d - 1], d)
 
-    for d in range(1, nh):
+    for d in farthest_first:
         share(d).start()
     keep = pltpu.make_async_copy(part, out_ref.at[x], load_sem.at[0])
     keep.start()
@@ -370,7 +375,7 @@
         out_specs=hbm,
         scratch_shapes=[
             pltpu.VMEM((1, n), jnp.int32),
-            pltpu.SMEM((1, 1), jnp.int32),
+            pltpu.SMEM((1,), jnp.int32),
             pltpu.VMEM((shard_rows, d_model), bf16),
             pltpu.VMEM(w_qkvu.shape, bf16),
             pltpu.VMEM((d_model, wq_width), bf16),
@@ -404,7 +409,7 @@
         compiler_params=pltpu.CompilerParams(
             collective_id=0, has_side_effects=True, vmem_limit_bytes=67_043_328
         ),
-    )(cand_ids, prefix_len.reshape(1, 1), key_cache, value_cache, item_table, w_qkvu, w_out)
+    )(cand_ids, prefix_len, key_cache, value_cache, item_table, w_qkvu, w_out)
     return jnp.sum(parts, axis=0)
 
 

time: 125 us -> 124 us (level)
  no operation moved by 1% of the time
where the time goes in v5:
time: 124 us
  Pallas kernels  122 us (98%)
  other arithmetic  1.3 us (1%)
    pallas_call x1, Pallas kernels, body(): pl.pallas_call(functools.partial(kernel, nz, nh, cap), out_shape=jax.Shap...  122 us

profile of v5, /device:TPU:97, one launch (start us, length us, event | category | flops | bytes accessed | tf_op | source)
XLA Modules:
  0.0 124.0 jit_solution(5689135919021317365)
XLA Ops:
  0.7 122.1 %shard_map.73 = f32[4,1,512]{2,1,0:T(1,128)} custom-call(s32[1,512]{1,0:T(1,128)} %ids_hbm.1, s32[1]{0:T(128)S(6)} %copy.8.len_hbm, bf16[1,512,256]{2,1,0:T(8,128)(2,1)} %k_hbm.1, bf16[1,512,256]{2,1,0:T(8,128)(2,1)} %v_hbm.1, bf16[512,1024]{1,0:T(8,128)(2,1)} %table_hbm.1, bf16[1024,2,4,128]{3,2,1,0:T(4,128)(2,1)} %wq_hbm.1, bf16[2,128,1024]{2,1,0:T(8,128)(2,1)} %wo_hbm.1), custom_call_target="tpu_custom_call" | custom-call | tf_op jit(solution)/shard_map/pallas_call | solution.py:371
  122.7 1.3 %reduce_sum.11 = f32[512]{0:T(512)} reduce(f32[4,1,512]{2,1,0:T(1,128)} %shard_map.73, f32[]{:T(128)} %constant.0.clone.1), dimensions={0,1}, to_apply=%region_0.0 | reduce | flops 1536 | bytes 10244 | tf_op jit(solution)/shard_map/reduce_sum | solution.py:413

commit v6 on v5

--- a/solution.py
+++ b/solution.py
@@ -174,9 +174,6 @@
     def half_out(d):
         return to_head(wo_hbm.at[c], wfull.at[x, c], w_send.at[d - 1], w_recv.at[d - 1], d)
 
-    for d in range(1, nh):
-        half_out(d).start()
-
     loads[0].wait()
 
     def answer(j, core):
@@ -200,16 +197,12 @@
         return carry
 
     lax.fori_loop(0, steps, serve, 0)
+    for d in range(1, nh):
+        half_out(d).start()
 
     def half_on(d):
         piece = wfull.at[(x + nh - d) % nh, c]
         return to_user(piece, piece, wp_send.at[d - 1], wp_recv.at[d - 1], partner)
-
-    for d in range(1, nh):
-        piece = wfull.at[(x + nh - d) % nh, c]
-        with jax.named_scope("w_wait"):
-            pltpu.make_async_copy(piece, piece, w_recv.at[d - 1]).wait()
-        half_on(d).start()
 
     for load in loads[1:5] + loads[6:]:
         load.wait()
@@ -279,6 +272,14 @@
                 pltpu.make_async_copy(mine, mine, row_recv.at[j]).wait()
             for d in farthest_first:
                 forward(j, d).start()
+
+        @pl.when(j == steps // 2)
+        def _():
+            for d in range(1, nh):
+                piece = wfull.at[(x + nh - d) % nh, c]
+                with jax.named_scope("w_wait"):
+                    pltpu.make_async_copy(piece, piece, w_recv.at[d - 1]).wait()
+                half_on(d).start()
 
         @pl.when(j >= LAG)
         def _():

time: 124 us -> 124 us (level)
  no operation moved by 1% of the time
where the time goes in v6:
time: 124 us
  Pallas kernels  122 us (98%)
  other arithmetic  1.3 us (1%)
    pallas_call x1, Pallas kernels, body(): pl.pallas_call(functools.partial(kernel, nz, nh, cap), out_shape=jax.Shap...  122 us

profile of v6, /device:TPU:97, one launch (start us, length us, event | category | flops | bytes accessed | tf_op | source)
XLA Modules:
  0.0 123.7 jit_solution(7040116376509326524)
XLA Ops:
  0.7 121.8 %shard_map.73 = f32[4,1,512]{2,1,0:T(1,128)} custom-call(s32[1,512]{1,0:T(1,128)} %ids_hbm.1, s32[1]{0:T(128)S(6)} %copy.8.len_hbm, bf16[1,512,256]{2,1,0:T(8,128)(2,1)} %k_hbm.1, bf16[1,512,256]{2,1,0:T(8,128)(2,1)} %v_hbm.1, bf16[512,1024]{1,0:T(8,128)(2,1)} %table_hbm.1, bf16[1024,2,4,128]{3,2,1,0:T(4,128)(2,1)} %wq_hbm.1, bf16[2,128,1024]{2,1,0:T(8,128)(2,1)} %wo_hbm.1), custom_call_target="tpu_custom_call" | custom-call | tf_op jit(solution)/shard_map/pallas_call | solution.py:372
  122.4 1.3 %reduce_sum.11 = f32[512]{0:T(512)} reduce(f32[4,1,512]{2,1,0:T(1,128)} %shard_map.73, f32[]{:T(128)} %constant.0.clone.1), dimensions={0,1}, to_apply=%region_0.0 | reduce | flops 1536 | bytes 10244 | tf_op jit(solution)/shard_map/reduce_sum | solution.py:414
